TPU v7x, 32 devices: a whole 2x2x4 slice. The times are simulated.
32 devices in a mesh: dp: 2 (over y), ctx: 8 (over z, x), tp: 2 (over core).
Axes of the slice: x: 2, y: 2, z: 4, core: 2. Of those that a mesh axis runs over, the one named last changes fastest.
Arguments:
- queries: bfloat16 [4, 1024, 4096], P('dp', 'ctx', 'tp'), may hold values from -6 to 6
- keys: bfloat16 [4, 1024, 512], P('dp', 'ctx', 'tp'), may hold values from -6 to 6
- values: bfloat16 [4, 1024, 512], P('dp', 'ctx', 'tp'), may hold values from -6 to 6
- output_gradient: bfloat16 [4, 1024, 4096], P('dp', 'ctx', 'tp'), may hold values from -6 to 6
- sinks: float32 [64], P('tp'), may hold values from -1 to 3
- doc_starts: int32 [4, 64], P('dp'), may hold values from 0 to 2048, as said below
- valid_counts: int32 [4, 8], P('dp'), may hold values from 64 to 128
Outputs:
- query_grad: bfloat16 [4, 1024, 4096], P('dp', 'ctx', 'tp')
- key_grad: bfloat16 [4, 1024, 512], P('dp', 'ctx', 'tp')
- value_grad: bfloat16 [4, 1024, 512], P('dp', 'ctx', 'tp')
- sink_grad: float32 [64], P('tp')
Inputs may be any that keep to these rules, and one draw needn't show every extreme that they name: `doc_starts`: each row is strictly increasing, begins with 0 and ends with 2048; a start at or past 1024 opens no document.
All inputs are finite; a program needn't handle non-finite values.
Results may differ from a plain program's by a relative error of at most 0.0093.
Values may be sent and summed in bfloat16 or wider, within the bound.
No kernel may reach another device: no remote copies, remote signals or barrier semaphores. Data moves between devices by JAX's collectives and lax.ppermute only.
A program may use at most 64 MiB of HBM per device.

v0:
```python
import math

import jax
import jax.numpy as jnp
from jax import lax
from jax.sharding import PartitionSpec as P

HEAD_DIMENSION = 64
WINDOW_LENGTH = 128


masked_score = -1e30


def passed_along(value, axis, steps):
    count = lax.axis_size(axis)
    first, last = (max(0, -steps), min(count, count - steps))
    return lax.ppermute(value, axis, [(source, source + steps) for source in range(first, last)])


def document_ids(starts, positions):
    return jnp.sum((starts[None, :] <= positions[:, None]).astype(jnp.int32), axis=1)


def key_valid_mask(counts, positions, block_rows):
    block_index = positions // block_rows
    offset = positions - block_index * block_rows
    matches = jnp.arange(counts.shape[0], dtype=jnp.int32)[None, :] == block_index[:, None]
    limits = jnp.sum(jnp.where(matches, counts[None, :], 0), axis=1)
    return offset < limits


def band_grads(
    query_tile_block,
    key_tile_block,
    value_tile_block,
    output_grad_block,
    query_pos,
    key_pos,
    query_doc,
    key_doc,
    key_valid,
    sink_logits,
):
    heads_kv = key_tile_block.shape[2]
    query_group_width = query_tile_block.shape[3]
    scaling = query_tile_block.shape[4] ** (-0.5)
    scores = (
        jnp.einsum(
            "nqhgd,nkhd->nhgqk",
            query_tile_block,
            key_tile_block,
            preferred_element_type=jnp.float32,
        )
        * scaling
    )
    allowed = (key_pos[:, None, :] <= query_pos[:, :, None]) & (
        query_pos[:, :, None] - key_pos[:, None, :] < WINDOW_LENGTH
    )
    allowed = allowed & (query_doc[:, :, None] == key_doc[:, None, :]) & key_valid[:, None, :]
    scores = jnp.where(allowed[:, None, None], scores, masked_score)
    sink_term = sink_logits.reshape(heads_kv, query_group_width)[None, :, :, None]
    maxima = jnp.maximum(jnp.max(scores, axis=-1), sink_term)
    powers = jnp.exp(scores - maxima[..., None])
    sink_exp = jnp.exp(sink_term - maxima)
    denominator = jnp.sum(powers, axis=-1) + sink_exp
    attend = powers / denominator[..., None]
    attend_low = attend.astype(jnp.bfloat16)
    context = jnp.einsum(
        "nhgqk,nkhd->nhgqd", attend_low, value_tile_block, preferred_element_type=jnp.float32
    )
    deltas = jnp.sum(
        jnp.transpose(output_grad_block, (0, 2, 3, 1, 4)).astype(jnp.float32) * context, axis=-1
    )
    grad_attend = jnp.einsum(
        "nqhgd,nkhd->nhgqk", output_grad_block, value_tile_block, preferred_element_type=jnp.float32
    )
    grad_score = attend * (grad_attend - deltas[..., None])
    score_low = grad_score.astype(jnp.bfloat16)
    query_grad = (
        jnp.einsum(
            "nhgqk,nkhd->nqhgd", score_low, key_tile_block, preferred_element_type=jnp.float32
        )
        * scaling
    )
    key_grad = (
        jnp.einsum(
            "nhgqk,nqhgd->nkhd", score_low, query_tile_block, preferred_element_type=jnp.float32
        )
        * scaling
    )
    value_grad = jnp.einsum(
        "nhgqk,nqhgd->nkhd", attend_low, output_grad_block, preferred_element_type=jnp.float32
    )
    sink_grad = -jnp.sum(sink_exp / denominator * deltas, axis=-1)
    return (
        query_grad,
        key_grad,
        value_grad,
        sink_grad.reshape(sink_grad.shape[0], heads_kv * query_group_width),
    )


def blockwise(entries, sink_logits):
    count_all = entries[0].shape[0]
    group_blocks = math.gcd(count_all, max(1, 512 // WINDOW_LENGTH))
    grouped = tuple(
        (
            member.reshape((count_all // group_blocks, group_blocks) + member.shape[1:])
            for member in entries
        )
    )

    def per_group(parts):
        return band_grads(*parts, sink_logits)

    results = lax.map(per_group, grouped)
    return tuple((member.reshape((count_all,) + member.shape[2:]) for member in results))


def block_facts(query_pos, key_pos, doc_starts, valid_counts, block_rows):
    collected = ([], [], [], [], [])
    for sequence_index in range(doc_starts.shape[0]):
        collected[0].append(query_pos)
        collected[1].append(key_pos)
        collected[2].append(
            document_ids(doc_starts[sequence_index], query_pos.reshape(-1)).reshape(query_pos.shape)
        )
        collected[3].append(
            document_ids(doc_starts[sequence_index], key_pos.reshape(-1)).reshape(key_pos.shape)
        )
        collected[4].append(
            key_valid_mask(valid_counts[sequence_index], key_pos.reshape(-1), block_rows).reshape(
                key_pos.shape
            )
        )
    return [jnp.concatenate(member, axis=0) for member in collected]


def local(queries, keys, values, output_gradient, sinks, doc_starts, valid_counts):
    seq_count, row_count, query_width = queries.shape
    kv_width = keys.shape[2]
    heads_kv = kv_width // HEAD_DIMENSION
    query_group_width = sinks.shape[0] // heads_kv
    block_tiles = row_count // WINDOW_LENGTH
    start_pos = lax.axis_index("ctx") * row_count
    halo_tails = passed_along((keys, values), "ctx", 1)

    def pair_rows(extended):
        shaped = extended.reshape(
            seq_count, block_tiles + 1, WINDOW_LENGTH, heads_kv, HEAD_DIMENSION
        )
        joined = jnp.concatenate([shaped[:, :-1], shaped[:, 1:]], axis=2)
        return joined.reshape(seq_count * block_tiles, 2 * WINDOW_LENGTH, heads_kv, HEAD_DIMENSION)

    query_lines = start_pos + jnp.arange(row_count, dtype=jnp.int32).reshape(
        block_tiles, WINDOW_LENGTH
    )
    key_lines = (
        start_pos - WINDOW_LENGTH + jnp.arange(row_count + WINDOW_LENGTH, dtype=jnp.int32)
    ).reshape(block_tiles + 1, WINDOW_LENGTH)
    key_lines = jnp.concatenate([key_lines[:-1], key_lines[1:]], axis=1)
    entries = [
        queries.reshape(
            seq_count * block_tiles, WINDOW_LENGTH, heads_kv, query_group_width, HEAD_DIMENSION
        ),
        pair_rows(jnp.concatenate([halo_tails[0], keys], axis=1)),
        pair_rows(jnp.concatenate([halo_tails[1], values], axis=1)),
        output_gradient.reshape(
            seq_count * block_tiles, WINDOW_LENGTH, heads_kv, query_group_width, HEAD_DIMENSION
        ),
    ] + block_facts(query_lines, key_lines, doc_starts, valid_counts, row_count)
    main_count = seq_count * block_tiles
    dq_all, dk_all, dv_all, sink_part = blockwise(entries, sinks)
    dk_main = dk_all.reshape(seq_count, block_tiles, 2 * WINDOW_LENGTH, kv_width)
    dv_main = dv_all.reshape(seq_count, block_tiles, 2 * WINDOW_LENGTH, kv_width)
    edge_keys, edge_values = (
        passed_along(dk_main[:, 0, :WINDOW_LENGTH].astype(jnp.bfloat16), "ctx", -1).astype(
            jnp.float32
        ),
        passed_along(dv_main[:, 0, :WINDOW_LENGTH].astype(jnp.bfloat16), "ctx", -1).astype(
            jnp.float32
        ),
    )
    key_total = dk_main[:, :, WINDOW_LENGTH:] + jnp.concatenate(
        [dk_main[:, 1:, :WINDOW_LENGTH], edge_keys[:, None]], axis=1
    )
    value_total = dv_main[:, :, WINDOW_LENGTH:] + jnp.concatenate(
        [dv_main[:, 1:, :WINDOW_LENGTH], edge_values[:, None]], axis=1
    )
    query_grad = dq_all.reshape(seq_count, row_count, query_width).astype(jnp.bfloat16)
    key_grad = key_total.reshape(seq_count, row_count, kv_width).astype(jnp.bfloat16)
    value_grad = value_total.reshape(seq_count, row_count, kv_width).astype(jnp.bfloat16)
    sink_grad = lax.psum(jnp.sum(sink_part, axis=0), ("dp", "ctx"))
    return (query_grad, key_grad, value_grad, sink_grad)


def solution(mesh):
    placed = (
        P("dp", "ctx", "tp"),
        P("dp", "ctx", "tp"),
        P("dp", "ctx", "tp"),
        P("dp", "ctx", "tp"),
        P("tp"),
        P("dp", None),
        P("dp", None),
    )
    return jax.shard_map(
        local,
        mesh=mesh,
        in_specs=placed,
        out_specs=(P("dp", "ctx", "tp"), P("dp", "ctx", "tp"), P("dp", "ctx", "tp"), P("tp")),
        check_vma=False,
    )
```

profile of v0, /device:TPU:0, one launch (start us, length us, event | category | flops | bytes accessed | tf_op | source)
XLA Modules:
  0.0 94.8 jit_solution(16104393274618011304)
XLA Ops:
  0.6 4.9 %collective-permute-start = (bf16[2,128,256]{2,1,0:T(8,128)(2,1)}, bf16[2,128,256]{2,1,0:T(8,128)(2,1)S(1)}, u32[]{:S(2)}, u32[]{:S(2)}) collective-permute-start(bf16[2,128,256]{2,1,0:T(8,128)(2,1)} %param.8), channel_id=1, source_target_pairs={{0,2},{2,4},{4,6},{6,8},{8,10},{10,12},{12,14},{1,3},{3,5},{5,7},{... | collective-permute-start | bytes 393224 | tf_op jit(solution)/shard_map/ppermute | solution.py:18
  5.5 4.1 %collective-permute-start.1 = (bf16[2,128,256]{2,1,0:T(8,128)(2,1)}, bf16[2,128,256]{2,1,0:T(8,128)(2,1)}, u32[]{:S(2)}, u32[]{:S(2)}) collective-permute-start(bf16[2,128,256]{2,1,0:T(8,128)(2,1)} %param.9), channel_id=1, source_target_pairs={{0,2},{2,4},{4,6},{6,8},{8,10},{10,12},{12,14},{1,3},{3,5},{5,7},{... | collective-permute-start | bytes 393224 | tf_op jit(solution)/shard_map/ppermute | solution.py:18
  9.7 0.8 slice_bitcast_fusion
  10.4 0.1 select_reduce_fusion.1
  10.5 0.8 slice_bitcast_fusion.2
  11.3 0.1 convert_reduce_fusion.1
  11.4 0.1 convert_reduce_fusion.3
  11.5 1.6 %copy.43 = bf16[2,128,2048]{1,2,0:T(8,128)(2,1)S(1)} copy(bf16[2,128,2048]{2,1,0:T(8,128)(2,1)} %param.7) | data formatting | bytes 2097152 | tf_op args[0]
  13.1 0.7 max.21
  13.9 1.6 %copy.47 = bf16[2,128,2048]{1,2,0:T(8,128)(2,1)S(1)} copy(bf16[2,128,2048]{2,1,0:T(8,128)(2,1)} %param.10) | data formatting | bytes 2097152 | tf_op args[3]
  15.6 0.3 fusion.17
  15.8 0.9 pad_maximum_fusion
  16.8 0.2 reshape.371
  17.0 0.2 fusion.29
  17.2 0.2 copy.69
  17.4 0.2 copy.70
  17.5 0.0 copy-start.5
  17.5 1.3 %fusion.4 = (f32[2,4,8,128]{3,2,1,0:T(8,128)S(1)}, f32[2,4,256,128,8]{3,2,4,1,0:T(8,128)S(1)}) fusion(pred[2,128,256]{1,2,0:T(8,128)(4,1)S(1)} %fusion.17, bf16[2,128,4,8,64]{1,4,3,2,0:T(8,128)(2,1)S(1)} %bitcast.104, bf16[2,1,128,4,64]{2,4,3,0,1:T(8,128)(2,1)S(1)} %copy.70, bf16[2,1,128,4,64]{2,4,3,0,1:T(8,128)(2,1)S(1)} %copy.69), kind=kOutput, calls=%fused_computation.7 | convolution fusion | flops 275243008 | bytes 9797632 | tf_op jit(solution)/shard_map/while/body/eval_jaxpr/nqhgd,nkhd->nhgqk/dot_general | solution.py:49
  18.9 0.1 broadcast_maximum_fusion
  18.9 3.1 %copy-done = f32[2,4,256,128,8]{3,2,4,1,0:T(8,128)} copy-done((f32[2,4,256,128,8]{3,2,4,1,0:T(8,128)}, f32[2,4,256,128,8]{3,2,4,1,0:T(8,128)S(1)}, u32[]{:S(2)}) %copy-start) | copy-done | bytes 8388632
  22.1 2.3 %fusion.3 = f32[2,4,8,128]{3,2,1,0:T(8,128)S(1)} fusion(f32[2,4,256,128,8]{3,2,4,1,0:T(8,128)S(1)} %get-tuple-element.80, f32[2,4,8,128]{3,2,1,0:T(8,128)S(1)} %broadcast_maximum_fusion, pred[2,128,256]{1,2,0:T(8,128)(4,1)S(1)} %fusion.17), kind=kLoop, calls=%fused_computation.6 | loop fusion | flops 8380416 | bytes 8519680 | tf_op jit(solution)/shard_map/while/body/eval_jaxpr/reduce_sum | solution.py:66
  24.3 0.7 fusion.21
  25.0 0.9 pad_maximum_fusion.1
  26.0 0.2 reshape.372
  26.2 0.2 fusion.30
  26.4 0.2 copy.71
  26.6 0.2 copy.72
  26.8 0.0 copy-start.6
  26.8 4.7 %fusion.6 = f32[2,4,256,64,1]{2,3,4,1,0:T(8,128)S(1)} fusion(bf16[2,128,4,8,64]{1,4,3,2,0:T(8,128)(2,1)S(1)} %bitcast.109, f32[2,4,256,128,8]{3,2,4,1,0:T(8,128)} %copy-done, f32[2,4,8,128]{3,2,1,0:T(8,128)} %fusion.21, f32[2,4,8,128]{3,2,1,0:T(8,128)} %copy-done.3, pred[2,128,256]{1,2,0:T(8,128)(4,1)S(1)} %fusion.17), kind=kOutput, calls=%fused_computation.11 | convolution fusion | flops 278921216 | bytes 10092544 | tf_op jit(solution)/shard_map/while/body/eval_jaxpr/nhgqk,nqhgd->nkhd/dot_general | solution.py:92
  31.4 0.0 copy-start.1
  31.5 0.8 copy.76
  32.3 1.7 %collective-permute-start.3 = (bf16[2,128,256]{2,1,0:T(8,128)(2,1)}, bf16[2,128,256]{2,1,0:T(8,128)(2,1)S(1)}, u32[]{:S(2)}, u32[]{:S(2)}) collective-permute-start(bf16[2,128,256]{2,1,0:T(8,128)(2,1)} %bitcast.114), channel_id=1, source_target_pairs={{2,0},{4,2},{6,4},{8,6},{10,8},{12,10},{14,12},{3,1},{5,3},{7,5},{... | collective-permute-start | bytes 393224 | tf_op jit(solution)/shard_map/ppermute | solution.py:18
  34.0 6.4 %fusion.5 = f32[2,4,8,128]{3,2,1,0:T(8,128)S(1)} fusion(bf16[2,128,4,8,64]{1,4,3,2,0:T(8,128)(2,1)S(1)} %bitcast.110, bf16[2,1,128,4,64]{2,4,3,0,1:T(8,128)(2,1)S(1)} %copy.72, bf16[2,1,128,4,64]{2,4,3,0,1:T(8,128)(2,1)S(1)} %copy.71, f32[2,4,256,128,8]{3,2,4,1,0:T(8,128)} %copy-done, f32[2,4,8,128]{3,2,1,0:T(8,128)S(1)} %copy-done.6, ...), kind=kOutput, calls=%fused_computation.9 | convolution fusion | flops 281010176 | bytes 9863168 | tf_op jit(solution)/shard_map/while/body/eval_jaxpr/nhgqk,nkhd->nhgqd/dot_general | solution.py:69
  40.5 3.0 %fusion.1 = bf16[2,4,8,128,256]{3,4,2,1,0:T(8,128)(2,1)S(1)} fusion(f32[2,4,8,128]{3,2,1,0:T(8,128)S(1)} %fusion.5, bf16[2,128,4,8,64]{1,4,3,2,0:T(8,128)(2,1)S(1)} %bitcast.111, bf16[2,1,128,4,64]{2,4,3,0,1:T(8,128)(2,1)S(1)} %copy.72, bf16[2,1,128,4,64]{2,4,3,0,1:T(8,128)(2,1)S(1)} %copy.71, f32[2,4,8,128]{3,2,1,0:T(8,128)S(1)} %copy-done.6, ...), kind=kOutput, calls=%fused_computation.2 | convolution fusion | flops 283639808 | bytes 14057472 | tf_op jit(solution)/shard_map/while/body/eval_jaxpr/nqhgd,nkhd->nhgqk/dot_general | solution.py:75
  43.5 0.0 copy-start.2
  43.5 1.4 %fusion.10 = f32[2,4,256,64]{2,3,1,0:T(8,128)S(1)} fusion(bf16[2,4,8,128,256]{3,4,2,1,0:T(8,128)(2,1)S(1)} %fusion.1, bf16[2,128,4,8,64]{1,4,3,2,0:T(8,128)(2,1)S(1)} %bitcast.105), kind=kOutput, calls=%fused_computation.16 | convolution fusion | flops 268566528 | bytes 5767168 | tf_op jit(solution)/shard_map/while/body/eval_jaxpr/nhgqk,nqhgd->nkhd/dot_general | solution.py:87
  44.9 0.8 multiply_convert_fusion
  45.8 0.2 multiply_reduce_fusion
  46.0 0.1 neg.9
  46.1 0.1 copy.75
  46.2 0.1 copy.73
  46.3 0.1 copy.74
  46.5 1.3 %collective-permute-start.2 = (bf16[2,128,256]{2,1,0:T(8,128)(2,1)S(1)}, bf16[2,128,256]{2,1,0:T(8,128)(2,1)S(1)}, u32[]{:S(2)}, u32[]{:S(2)}) collective-permute-start(bf16[2,128,256]{2,1,0:T(8,128)(2,1)S(1)} %bitcast.115), channel_id=1, source_target_pairs={{2,0},{4,2},{6,4},{8,6},{10,8},{12,10},{14,12},{3,1},{5,3},{7,5},{... | collective-permute-start | bytes 393224 | tf_op jit(solution)/shard_map/ppermute | solution.py:18
  47.8 1.3 %copy.56 = bf16[2,128,2048]{2,1,0:T(8,128)(2,1)} copy(bf16[2,128,2048]{1,2,0:T(8,128)(2,1)S(1)} %bitcast.106) | data formatting | bytes 2097152
  49.1 44.4 %psum.7 = f32[32]{0:T(128)} all-reduce(f32[32]{0:T(128)S(1)} %neg.9), channel_id=1, replica_groups=mesh['dp'=2,'ctx'=8,'tp'=2] {'dp','ctx'}, use_global_device_ids=true, to_apply=%region_10.11 | all-reduce | flops 32 | bytes 256 | tf_op jit(solution)/shard_map/psum | solution.py:194
  93.4 0.7 fusion.20
  94.1 0.0 collective-permute-done.2
  94.1 0.7 fusion.19
  (33 shorter events, 0.2 us)
Async XLA Ops:
  0.6 15.2 %collective-permute-start = (bf16[2,128,256]{2,1,0:T(8,128)(2,1)}, bf16[2,128,256]{2,1,0:T(8,128)(2,1)S(1)}, u32[]{:S(2)}, u32[]{:S(2)}) collective-permute-start(bf16[2,128,256]{2,1,0:T(8,128)(2,1)} %param.8), channel_id=1, source_target_pairs={{0,2},{2,4},{4,6},{6,8},{8,10},{10,12},{12,14},{1,3},{3,5},{5,7},{... | collective-permute-start | bytes 393224 | tf_op jit(solution)/shard_map/ppermute | solution.py:18
  5.5 19.5 %collective-permute-start.1 = (bf16[2,128,256]{2,1,0:T(8,128)(2,1)}, bf16[2,128,256]{2,1,0:T(8,128)(2,1)}, u32[]{:S(2)}, u32[]{:S(2)}) collective-permute-start(bf16[2,128,256]{2,1,0:T(8,128)(2,1)} %param.9), channel_id=1, source_target_pairs={{0,2},{2,4},{4,6},{6,8},{8,10},{10,12},{12,14},{1,3},{3,5},{5,7},{... | collective-permute-start | bytes 393224 | tf_op jit(solution)/shard_map/ppermute | solution.py:18
  17.5 7.5 %copy-start.5 = (bf16[2,128,256]{2,1,0:T(8,128)(2,1)S(1)}, bf16[2,128,256]{2,1,0:T(8,128)(2,1)}, u32[]{:S(2)}) copy-start(bf16[2,128,256]{2,1,0:T(8,128)(2,1)} %param.9) | copy-start | bytes 393220
  18.9 3.2 %copy-start = (f32[2,4,256,128,8]{3,2,4,1,0:T(8,128)}, f32[2,4,256,128,8]{3,2,4,1,0:T(8,128)S(1)}, u32[]{:S(2)}) copy-start(f32[2,4,256,128,8]{3,2,4,1,0:T(8,128)S(1)} %get-tuple-element.80) | copy-start | bytes 25165828
  18.9 6.1 %copy-start.3 = (f32[2,4,8,128]{3,2,1,0:T(8,128)}, f32[2,4,8,128]{3,2,1,0:T(8,128)S(1)}, u32[]{:S(2)}) copy-start(f32[2,4,8,128]{3,2,1,0:T(8,128)S(1)} %broadcast_maximum_fusion) | copy-start | bytes 98308
  26.7 7.3 %copy-start.4 = (f32[2,4,8,128]{3,2,1,0:T(8,128)S(1)}, f32[2,4,8,128]{3,2,1,0:T(8,128)}, u32[]{:S(2)}) copy-start(f32[2,4,8,128]{3,2,1,0:T(8,128)} %copy-done.3) | copy-start | bytes 98308
  26.8 7.3 %copy-start.6 = (f32[2,4,8,128]{3,2,1,0:T(8,128)S(1)}, f32[2,4,8,128]{3,2,1,0:T(8,128)}, u32[]{:S(2)}) copy-start(f32[2,4,8,128]{3,2,1,0:T(8,128)} %fusion.21) | copy-start | bytes 98308
  31.4 9.0 %copy-start.1 = (f32[2,4,256,64,1]{2,3,4,1,0:T(8,128)}, f32[2,4,256,64,1]{2,3,4,1,0:T(8,128)S(1)}, u32[]{:S(2)}) copy-start(f32[2,4,256,64,1]{2,3,4,1,0:T(8,128)S(1)} %fusion.6) | copy-start | bytes 1572868
  32.3 8.2 %slice-start = ((s8[8388608]{0:T(1024)(128)(4,1)}), s8[4194304]{0:T(1024)(128)(4,1)S(1)}, s32[]{:S(2)}) async-start(s8[8388608]{0:T(1024)(128)(4,1)} %bitcast.102), calls=%async_computation | async-start | bytes 8388608
  32.3 8.2 %slice-start.1 = ((s8[8388608]{0:T(1024)(128)(4,1)}), s8[4194304]{0:T(1024)(128)(4,1)S(1)}, s32[]{:S(2)}) async-start(s8[8388608]{0:T(1024)(128)(4,1)} %bitcast.102), calls=%async_computation.1 | async-start | bytes 8388608
  32.3 61.2 %collective-permute-start.3 = (bf16[2,128,256]{2,1,0:T(8,128)(2,1)}, bf16[2,128,256]{2,1,0:T(8,128)(2,1)S(1)}, u32[]{:S(2)}, u32[]{:S(2)}) collective-permute-start(bf16[2,128,256]{2,1,0:T(8,128)(2,1)} %bitcast.114), channel_id=1, source_target_pairs={{2,0},{4,2},{6,4},{8,6},{10,8},{12,10},{14,12},{3,1},{5,3},{7,5},{... | collective-permute-start | bytes 393224 | tf_op jit(solution)/shard_map/ppermute | solution.py:18
  43.5 2.2 %copy-start.2 = (f32[2,4,256,64,1]{2,3,4,1,0:T(8,128)S(1)}, f32[2,4,256,64,1]{2,3,4,1,0:T(8,128)}, u32[]{:S(2)}) copy-start(f32[2,4,256,64,1]{2,3,4,1,0:T(8,128)} %copy-done.1) | copy-start | bytes 1572868
  46.5 47.7 %collective-permute-start.2 = (bf16[2,128,256]{2,1,0:T(8,128)(2,1)S(1)}, bf16[2,128,256]{2,1,0:T(8,128)(2,1)S(1)}, u32[]{:S(2)}, u32[]{:S(2)}) collective-permute-start(bf16[2,128,256]{2,1,0:T(8,128)(2,1)S(1)} %bitcast.115), channel_id=1, source_target_pairs={{2,0},{4,2},{6,4},{8,6},{10,8},{12,10},{14,12},{3,1},{5,3},{7,5},{... | collective-permute-start | bytes 393224 | tf_op jit(solution)/shard_map/ppermute | solution.py:18
where the time goes:
time: 95.1 us; the launch traced here: 94.8 us
  blocking collectives  44.4 us (47%)
  matrix products  17.6 us (19%)
  local copies, waits for them, and re-layouts  12.8 us (13%)
  starting transfers between devices  12 us (13%)
  other arithmetic  7.06 us (7%)
  between operations  1.01 us (1%)
    psum x1, blocking collectives, local(): sink_grad = lax.psum(jnp.sum(sink_part, axis=0), ('dp', 'ctx'))  44.4 us
    ppermute x4, starting transfers between devices, passed_along(): lax.ppermute(value, axis, [(source, source + steps) for source in range(f...  12 us
    unnamed x29, local copies, waits for them, and re-layouts  9.51 us
    dot_general x1, matrix products, band_grads(): jnp.einsum('nhgqk,nkhd->nhgqd', attend_low, value_tile_block, preferred_e...  6.43 us
    dot_general x1, matrix products, band_grads(): jnp.einsum('nhgqk,nqhgd->nkhd', attend_low, output_grad_block, preferred_...  4.66 us
    dot_general x1, matrix products, band_grads(): jnp.einsum('nqhgd,nkhd->nhgqk', output_grad_block, value_tile_block, pref...  3 us
    reduce_sum x1, other arithmetic, band_grads(): denominator = jnp.sum(powers, axis=-1) + sink_exp  2.26 us
  transfers between devices with their start and end apart: 4, of which 0 were waited for; matrix products, arithmetic and copies ran while one was open for 28% of the time, Pallas kernels for 0%

commit v1 on v0

v1 whole, which is shorter than its diff:
```python
import functools
import math

import jax
import jax.numpy as jnp
from jax import lax
from jax.experimental import pallas as pl
from jax.experimental.pallas import tpu as pltpu
from jax.sharding import PartitionSpec as P

HEAD_DIMENSION = 64
WINDOW_LENGTH = 128
LANES = 128

masked_score = -1e30

dot_nt = functools.partial(
    lax.dot_general,
    dimension_numbers=(((1,), (1,)), ((), ())),
    preferred_element_type=jnp.float32,
)
dot_nn = functools.partial(
    lax.dot_general,
    dimension_numbers=(((1,), (0,)), ((), ())),
    preferred_element_type=jnp.float32,
)


def passed_along(value, axis, steps):
    count = lax.axis_size(axis)
    first, last = (max(0, -steps), min(count, count - steps))
    return lax.ppermute(value, axis, [(source, source + steps) for source in range(first, last)])


def total_over(value, axes):
    for axis in axes:
        count = lax.axis_size(axis)
        if count & (count - 1):
            value = lax.psum(value, axis)
            continue
        step = 1
        while step < count:
            value = value + lax.ppermute(value, axis, [(i, i ^ step) for i in range(count)])
            step *= 2
    return value


def lane_half():
    return lax.broadcasted_iota(jnp.int32, (WINDOW_LENGTH, LANES), 1) < HEAD_DIMENSION


def half_pair(tile, which):
    low = lane_half()
    wide = tile.astype(jnp.float32)
    if which == 0:
        lo = jnp.where(low, wide, 0.0)
        hi = pltpu.roll(lo, HEAD_DIMENSION, 1)
    else:
        hi = jnp.where(low, 0.0, wide)
        lo = pltpu.roll(hi, HEAD_DIMENSION, 1)
    return lo.astype(jnp.bfloat16), hi.astype(jnp.bfloat16)


def write_masks(starts_ref, counts_ref, seq, block, own_bias, prev_bias):
    base = block * WINDOW_LENGTH
    query = base + lax.broadcasted_iota(jnp.int32, (8, LANES), 1)
    oldest = jnp.zeros((8, LANES), jnp.int32)
    for entry in range(starts_ref.shape[1]):
        start = starts_ref[seq, entry]
        oldest = jnp.maximum(oldest, jnp.where(start <= query, start, 0))
    oldest = jnp.broadcast_to(oldest[:1], (WINDOW_LENGTH, LANES))
    key_row = lax.broadcasted_iota(jnp.int32, (WINDOW_LENGTH, LANES), 0)
    query_lane = lax.broadcasted_iota(jnp.int32, (WINDOW_LENGTH, LANES), 1)
    own_limit = counts_ref[seq, block]
    prev_limit = counts_ref[seq, jnp.maximum(block - 1, 0)]
    own = (key_row <= query_lane) & (key_row + base >= oldest) & (key_row < own_limit)
    prev = (
        (key_row > query_lane)
        & (key_row + (base - WINDOW_LENGTH) >= oldest)
        & (key_row < prev_limit)
    )
    own_bias[...] = jnp.where(own, 0.0, masked_score)
    prev_bias[...] = jnp.where(prev, 0.0, masked_score)


def twice(tile):
    return jnp.concatenate([tile, tile], axis=1)


def grads_kernel(
    sinks_ref,
    starts_ref,
    counts_ref,
    q_ref,
    g_ref,
    k_ref,
    v_ref,
    hk_ref,
    hv_ref,
    dq_ref,
    own_ref,
    prev_ref,
    sink_ref,
    own_bias,
    prev_bias,
    sink_rows,
    *,
    group,
):
    seq, pair = pl.program_id(0), pl.program_id(1)
    pairs = pl.num_programs(1)
    block = lax.axis_index("ctx")
    scaling = HEAD_DIMENSION**-0.5
    to_exp2 = scaling * math.log2(math.e)

    @pl.when(pair == 0)
    def _():
        write_masks(starts_ref, counts_ref, seq, block, own_bias, prev_bias)

    @pl.when((seq == 0) & (pair == 0))
    def _():
        sink_rows[...] = jnp.zeros_like(sink_rows)

    bias_own, bias_prev = twice(own_bias[...]), twice(prev_bias[...])
    key_row = lax.broadcasted_iota(jnp.int32, (WINDOW_LENGTH, 2 * LANES), 0)
    query_lane = lax.broadcasted_iota(jnp.int32, (WINDOW_LENGTH, 2 * LANES), 1) % LANES
    lower = key_row <= query_lane
    lower_low = lower.astype(jnp.float32).astype(jnp.bfloat16)
    first_head = lax.broadcasted_iota(jnp.int32, (1, 2 * LANES), 1) < LANES
    low = jnp.concatenate([lane_half(), lane_half()], axis=0)

    k_own, v_own = k_ref[0], v_ref[0]
    k_prev, v_prev = hk_ref[0], hv_ref[0]
    kt_own, kt_prev = k_own.T, k_prev.T
    sums = []
    for which in range(2):
        keys = jnp.concatenate(
            [*half_pair(k_own, which), *half_pair(k_prev, which)], axis=0
        )
        vals = jnp.concatenate(
            [*half_pair(v_own, which), *half_pair(v_prev, which)], axis=0
        )
        rows = slice(which * HEAD_DIMENSION, (which + 1) * HEAD_DIMENSION)
        keys_t = jnp.concatenate([kt_own[rows], kt_prev[rows]], axis=1)
        totals = [[[], []], [[], []]]
        for quad in range(group // 4):
            at = (which * group + quad * 4) * HEAD_DIMENSION
            spans = (slice(at, at + LANES), slice(at + LANES, at + 2 * LANES))
            q_cat = jnp.concatenate([q_ref[0, :, span] for span in spans], axis=0)
            g_cat = jnp.concatenate([g_ref[0, :, span] for span in spans], axis=0)
            scores = dot_nt(keys, q_cat)
            dprobs = dot_nt(vals, g_cat)
            dq_parts = []
            for half in range(2):
                own_rows = slice(half * WINDOW_LENGTH, (half + 1) * WINDOW_LENGTH)
                prev_rows = slice((half + 2) * WINDOW_LENGTH, (half + 3) * WINDOW_LENGTH)
                head = pair * 2 * group + which * group + quad * 4 + half
                sink = jnp.where(first_head, sinks_ref[head], sinks_ref[head + 2]) / scaling
                s = jnp.maximum(scores[own_rows] + bias_own, scores[prev_rows] + bias_prev)
                top = jnp.maximum(jnp.max(s, axis=0, keepdims=True), sink)
                power = jnp.exp2((s - top) * to_exp2)
                sink_power = jnp.exp2((sink - top) * to_exp2)
                inverse = 1.0 / (jnp.sum(power, axis=0, keepdims=True) + sink_power)
                dprob = jnp.where(lower, dprobs[own_rows], dprobs[prev_rows])
                delta = jnp.sum(power * dprob, axis=0, keepdims=True) * inverse
                prob = power * inverse
                dscore = prob * (dprob - delta)
                sink_term = sink_power * inverse * delta
                sink_rows[pl.ds(head, 1), :] += sink_term[:, :LANES]
                sink_rows[pl.ds(head + 2, 1), :] += sink_term[:, LANES:]
                prob_low = prob.astype(jnp.bfloat16)
                dscore_low = dscore.astype(jnp.bfloat16)
                prob_own = prob_low * lower_low
                dscore_own = dscore_low * lower_low
                prob_both = jnp.concatenate([prob_own, prob_low - prob_own], axis=0)
                dscore_both = jnp.concatenate([dscore_own, dscore_low - dscore_own], axis=0)
                dq_parts.append(dot_nn(keys_t, dscore_both) * scaling)
                totals[0][half].append((dscore_both, q_cat))
                totals[1][half].append((prob_both, g_cat))
            for part in range(2):
                lanes = slice(part * LANES, (part + 1) * LANES)
                tile = jnp.concatenate([dq_parts[0][:, lanes], dq_parts[1][:, lanes]], axis=0)
                dq_ref[0, :, spans[part]] = tile.astype(jnp.bfloat16).T
        sums.append(
            [
                [
                    dot_nn(
                        jnp.concatenate([left for left, _ in totals[kind][half]], axis=1),
                        jnp.concatenate([right for _, right in totals[kind][half]], axis=0),
                    )
                    for half in range(2)
                ]
                for kind in range(2)
            ]
        )
    for kind, factor in ((0, scaling), (1, 1.0)):
        (lo0, hi0), (lo1, hi1) = sums[0][kind], sums[1][kind]
        grad = jnp.where(low, lo0, hi1) + pltpu.roll(
            jnp.where(low, lo1, hi0), HEAD_DIMENSION, 1
        )
        grad = grad * factor
        own_ref[kind, 0] = grad[:WINDOW_LENGTH]
        prev_ref[kind, 0] = grad[WINDOW_LENGTH:].astype(jnp.bfloat16)

    @pl.when((seq == pl.num_programs(0) - 1) & (pair == pairs - 1))
    def _():
        sink_ref[...] = -jnp.sum(sink_rows[...].T, axis=0, keepdims=True)


def local(queries, keys, values, output_gradient, sinks, doc_starts, valid_counts):
    seq_count, row_count, query_width = queries.shape
    kv_width = keys.shape[2]
    heads_kv = kv_width // HEAD_DIMENSION
    head_count = sinks.shape[0]
    group = head_count // heads_kv
    pairs = heads_kv // 2
    assert row_count == WINDOW_LENGTH
    halo = passed_along(jnp.stack([keys, values]), "ctx", 1)
    wide = 2 * group * HEAD_DIMENSION
    smem = pl.BlockSpec(memory_space=pltpu.SMEM)
    wide_spec = pl.BlockSpec((1, row_count, wide), lambda b, p: (b, 0, p))
    kv_spec = pl.BlockSpec((1, row_count, LANES), lambda b, p: (b, 0, p))
    both_spec = pl.BlockSpec((2, 1, row_count, LANES), lambda b, p: (0, b, 0, p))
    padded_heads = -(-head_count // LANES) * LANES
    query_grad, own, prev, sink_part = pl.pallas_call(
        functools.partial(grads_kernel, group=group),
        grid=(seq_count, pairs),
        in_specs=[smem, smem, smem, wide_spec, wide_spec, kv_spec, kv_spec]
        + [
            pl.BlockSpec((None, 1, row_count, LANES), lambda b, p, kind=kind: (kind, b, 0, p))
            for kind in range(2)
        ],
        out_specs=[
            wide_spec,
            both_spec,
            both_spec,
            pl.BlockSpec((1, padded_heads), lambda b, p: (0, 0)),
        ],
        out_shape=[
            jax.ShapeDtypeStruct(queries.shape, jnp.bfloat16),
            jax.ShapeDtypeStruct((2,) + keys.shape, jnp.float32),
            jax.ShapeDtypeStruct((2,) + keys.shape, jnp.bfloat16),
            jax.ShapeDtypeStruct((1, padded_heads), jnp.float32),
        ],
        scratch_shapes=[
            pltpu.VMEM((WINDOW_LENGTH, LANES), jnp.float32),
            pltpu.VMEM((WINDOW_LENGTH, LANES), jnp.float32),
            pltpu.VMEM((padded_heads, LANES), jnp.float32),
        ],
    )(
        sinks,
        doc_starts,
        valid_counts,
        queries,
        output_gradient,
        keys,
        values,
        halo,
        halo,
    )
    edge = passed_along(prev, "ctx", -1)
    total = (own + edge.astype(jnp.float32)).astype(jnp.bfloat16)
    sink_grad = total_over(sink_part[0, :head_count], ("dp", "ctx"))
    return (query_grad, total[0], total[1], sink_grad)


def solution(mesh):
    placed = (
        P("dp", "ctx", "tp"),
        P("dp", "ctx", "tp"),
        P("dp", "ctx", "tp"),
        P("dp", "ctx", "tp"),
        P("tp"),
        P("dp", None),
        P("dp", None),
    )
    return jax.shard_map(
        local,
        mesh=mesh,
        in_specs=placed,
        out_specs=(P("dp", "ctx", "tp"), P("dp", "ctx", "tp"), P("dp", "ctx", "tp"), P("tp")),
        check_vma=False,
    )
```

time: 95.1 us -> 46.4 us (0.49)
  blocking collectives: 44.4 us -> 0 us
  matrix products: 17.6 us -> 0 us
  waiting for transfers between devices: 0.01 us -> 12.7 us
  Pallas kernels: 0 us -> 11.8 us
  local copies, waits for them, and re-layouts: 12.8 us -> 1.43 us
  starting transfers between devices: 12 us -> 16.9 us
  other arithmetic: 7.06 us -> 2.63 us
    psum x1 -> x0, blocking collectives: 44.4 us -> none  [local(): sink_grad = lax.psum(jnp.sum(sink_part, axis=0), ('dp', 'ctx'))]
    dot_general x6 -> x0, matrix products: 17.6 us -> none  [the longest x1 6.43 us: band_grads(): jnp.einsum('nhgqk,nkhd->nhgqd', attend_low, value_tile_block, preferred_e...]
    pallas_call x0 -> x1, Pallas kernels: none -> 11.8 us  [local(): pl.pallas_call(functools.partial(grads_kernel, group=group), grid=(seq_co...]
    ppermute x0 -> x4, starting transfers between devices: none -> 10.7 us  [total_over(): lax.ppermute(value, axis, [(i, i ^ step) for i in range(count)])]
    unnamed x29 -> x4, local copies, waits for them, and re-layouts: 9.51 us -> 0.71 us
    ppermute x0 -> x4, waiting for transfers between devices: none -> 7.2 us  [total_over(): lax.ppermute(value, axis, [(i, i ^ step) for i in range(count)])]
    ppermute x4 -> x2, starting transfers between devices: 12 us -> 6.18 us  [passed_along(): lax.ppermute(value, axis, [(source, source + steps) for source in range(f...]
    ppermute x4 -> x2, waiting for transfers between devices: 0.01 us -> 5.53 us  [passed_along(): lax.ppermute(value, axis, [(source, source + steps) for source in range(f...]
  transfers between devices with their start and end apart: 4 -> 6, of which waited for: 0 -> 5; matrix products, arithmetic and copies ran while one was open for 28% -> 1% of each run, Pallas kernels for 0% -> 0%
where the time goes in v1:
time: 46.4 us; the launch traced here: 46.2 us
  starting transfers between devices  16.9 us (36%)
  waiting for transfers between devices  12.7 us (27%)
  Pallas kernels  11.8 us (25%)
  other arithmetic  2.63 us (6%)
  local copies, waits for them, and re-layouts  1.43 us (3%)
  between operations  0.69 us (1%)
    pallas_call x1, Pallas kernels, local(): pl.pallas_call(functools.partial(grads_kernel, group=group), grid=(seq_co...  11.8 us
    ppermute x4, starting transfers between devices, total_over(): lax.ppermute(value, axis, [(i, i ^ step) for i in range(count)])  10.7 us
    ppermute x4, waiting for transfers between devices, total_over(): lax.ppermute(value, axis, [(i, i ^ step) for i in range(count)])  7.2 us
    ppermute x2, starting transfers between devices, passed_along(): lax.ppermute(value, axis, [(source, source + steps) for source in range(f...  6.18 us
    ppermute x2, waiting for transfers between devices, passed_along(): lax.ppermute(value, axis, [(source, source + steps) for source in range(f...  5.53 us
    convert_element_type x1, other arithmetic, local(): total = (own + edge.astype(jnp.float32)).astype(jnp.bfloat16)  1.11 us
    another operation x1, other arithmetic, local(): halo = passed_along(jnp.stack([keys, values]), 'ctx', 1)  1 us
  transfers between devices with their start and end apart: 6, of which 5 were waited for; matrix products, arithmetic and copies ran while one was open for 1% of the time, Pallas kernels for 0%

profile of v1, /device:TPU:0, one launch (start us, length us, event | category | flops | bytes accessed | tf_op | source)
XLA Modules:
  0.0 46.2 jit_solution(5885568801324219442)
XLA Ops:
  0.6 1.0 %pad_maximum_fusion = bf16[2,2,128,256]{3,2,1,0:T(8,128)(2,1)S(1)} fusion(bf16[1,2,128,256]{3,2,1,0:T(8,128)(2,1)} %bitcast.11, bf16[1,2,128,256]{3,2,1,0:T(8,128)(2,1)} %bitcast.10), kind=kLoop, calls=%fused_computation.1 | loop fusion | flops 131072 | bytes 524288 | tf_op jit(solution)/shard_map/stack | solution.py:218
  1.6 4.9 %collective-permute-start = (bf16[2,2,128,256]{3,2,1,0:T(8,128)(2,1)S(1)}, bf16[2,2,128,256]{3,2,1,0:T(8,128)(2,1)S(1)}, u32[]{:S(2)}, u32[]{:S(2)}) collective-permute-start(bf16[2,2,128,256]{3,2,1,0:T(8,128)(2,1)S(1)} %pad_maximum_fusion), channel_id=1, source_target_pairs={{0,2},{2,4},{4,6},{6,8},{8,10},{10,12},{12,14},{1,3},{3,5},{5,7},{... | collective-permute-start | bytes 786440 | tf_op jit(solution)/shard_map/ppermute | solution.py:32
  6.5 5.5 %collective-permute-done.hk_ref.hv_ref = bf16[2,2,128,256]{3,2,1,0:T(8,128)(2,1)S(1)} collective-permute-done((bf16[2,2,128,256]{3,2,1,0:T(8,128)(2,1)S(1)}, bf16[2,2,128,256]{3,2,1,0:T(8,128)(2,1)S(1)}, u32[]{:S(2)}, u32[]{:S(2)}) %collective-permute-start) | collective-permute-done | bytes 262176 | tf_op jit(solution)/shard_map/ppermute | solution.py:32
  12.1 0.0 copy-start
  12.1 0.7 %copy-done = bf16[2,2,128,256]{3,2,1,0:T(8,128)(2,1)} copy-done((bf16[2,2,128,256]{3,2,1,0:T(8,128)(2,1)}, bf16[2,2,128,256]{3,2,1,0:T(8,128)(2,1)S(1)}, u32[]{:S(2)}) %copy-start) | copy-done | bytes 262168
  12.8 11.8 %shard_map.102 = (bf16[2,128,2048]{2,1,0:T(8,128)(2,1)}, f32[2,2,128,256]{3,2,1,0:T(8,128)}, bf16[2,2,128,256]{3,2,1,0:T(8,128)(2,1)}, f32[1,128]{1,0:T(1,128)}) custom-call(f32[32]{0:T(128)} %sinks_ref.1, s32[2,64]{1,0:T(2,128)} %starts_ref.1, s32[2,8]{1,0:T(2,128)} %counts_ref.1, bf16[2,128,2048]{2,1,0:T(8,128)(2,1)} %q_ref.1, ...), custom_call_target="tpu_custom_call" | custom-call | tf_op jit(solution)/shard_map/pallas_call | solution.py:225
  24.6 0.0 copy-start.1
  24.6 1.3 %collective-permute-start.1 = (bf16[2,2,128,256]{3,2,1,0:T(8,128)(2,1)}, bf16[2,2,128,256]{3,2,1,0:T(8,128)(2,1)S(1)}, u32[]{:S(2)}, u32[]{:S(2)}) collective-permute-start(bf16[2,2,128,256]{3,2,1,0:T(8,128)(2,1)} %get-tuple-element.10), channel_id=1, source_target_pairs={{2,0},{4,2},{6,4},{8,6},{10,8},{12,10},{14,12},{3,1},{5,3},{7,5},{... | collective-permute-start | bytes 786440 | tf_op jit(solution)/shard_map/ppermute | solution.py:32
  25.9 0.0 copy-done.1
  25.9 1.6 %collective-permute-start.2 = (f32[32]{0:T(128)S(1)}, f32[32]{0:T(128)S(1)}, u32[]{:S(2)}, u32[]{:S(2)}) collective-permute-start(f32[32]{0:T(128)S(1)} %slice_bitcast_fusion.2), channel_id=1, source_target_pairs={{0,16},{16,0},{1,17},{17,1},{2,18},{18,2},{3,19},{19,3},{4,20},{20... | collective-permute-start | bytes 392 | tf_op jit(solution)/shard_map/ppermute | solution.py:43
  27.5 2.0 %collective-permute-done.2 = f32[32]{0:T(128)S(1)} collective-permute-done((f32[32]{0:T(128)S(1)}, f32[32]{0:T(128)S(1)}, u32[]{:S(2)}, u32[]{:S(2)}) %collective-permute-start.2) | collective-permute-done | bytes 160 | tf_op jit(solution)/shard_map/ppermute | solution.py:43
  29.5 3.1 %collective-permute-start.3 = (f32[32]{0:T(128)S(1)}, f32[32]{0:T(128)S(1)}, u32[]{:S(2)}, u32[]{:S(2)}) collective-permute-start(f32[32]{0:T(128)S(1)} %fusion), channel_id=1, source_target_pairs={{0,2},{2,0},{4,6},{6,4},{8,10},{10,8},{12,14},{14,12},{1,3},{3,1},... | collective-permute-start | bytes 392 | tf_op jit(solution)/shard_map/ppermute | solution.py:43
  32.7 2.1 %collective-permute-done.3 = f32[32]{0:T(128)S(1)} collective-permute-done((f32[32]{0:T(128)S(1)}, f32[32]{0:T(128)S(1)}, u32[]{:S(2)}, u32[]{:S(2)}) %collective-permute-start.3) | collective-permute-done | bytes 160 | tf_op jit(solution)/shard_map/ppermute | solution.py:43
  34.7 3.0 %collective-permute-start.4 = (f32[32]{0:T(128)S(1)}, f32[32]{0:T(128)S(1)}, u32[]{:S(2)}, u32[]{:S(2)}) collective-permute-start(f32[32]{0:T(128)S(1)} %add.17), channel_id=1, source_target_pairs={{0,4},{2,6},{4,0},{6,2},{8,12},{10,14},{12,8},{14,10},{1,5},{3,7},... | collective-permute-start | bytes 392 | tf_op jit(solution)/shard_map/ppermute | solution.py:43
  37.7 1.5 %collective-permute-done.4 = f32[32]{0:T(128)S(1)} collective-permute-done((f32[32]{0:T(128)S(1)}, f32[32]{0:T(128)S(1)}, u32[]{:S(2)}, u32[]{:S(2)}) %collective-permute-start.4) | collective-permute-done | bytes 160 | tf_op jit(solution)/shard_map/ppermute | solution.py:43
  39.2 3.0 %collective-permute-start.5 = (f32[32]{0:T(128)S(1)}, f32[32]{0:T(128)S(1)}, u32[]{:S(2)}, u32[]{:S(2)}) collective-permute-start(f32[32]{0:T(128)S(1)} %add.18), channel_id=1, source_target_pairs={{0,8},{2,10},{4,12},{6,14},{8,0},{10,2},{12,4},{14,6},{1,9},{3,11}... | collective-permute-start | bytes 392 | tf_op jit(solution)/shard_map/ppermute | solution.py:43
  42.3 1.5 %collective-permute-done.5 = f32[32]{0:T(128)S(1)} collective-permute-done((f32[32]{0:T(128)S(1)}, f32[32]{0:T(128)S(1)}, u32[]{:S(2)}, u32[]{:S(2)}) %collective-permute-start.5) | collective-permute-done | bytes 160 | tf_op jit(solution)/shard_map/ppermute | solution.py:43
  43.8 0.5 %add.19 = f32[32]{0:T(128)} add(f32[32]{0:T(128)S(1)} %add.18, f32[32]{0:T(128)S(1)} %collective-permute-done.5) | non-fusion elementwise | flops 32 | bytes 384 | tf_op jit(solution)/shard_map/add | solution.py:43
  44.3 0.0 collective-permute-done.1
  44.3 1.1 %add_convert_fusion = bf16[2,2,128,256]{3,2,1,0:T(8,128)(2,1)S(1)} fusion(f32[2,2,128,256]{3,2,1,0:T(8,128)} %get-tuple-element.9, bf16[2,2,128,256]{3,2,1,0:T(8,128)(2,1)S(1)} %collective-permute-done.1), kind=kLoop, calls=%fused_computation | loop fusion | flops 393216 | bytes 1048576 | tf_op jit(solution)/shard_map/convert_element_type | solution.py:262
  45.4 0.7 %slice_bitcast_fusion = (bf16[2,128,256]{2,1,0:T(8,128)(2,1)}, bf16[2,128,256]{2,1,0:T(8,128)(2,1)}) fusion(bf16[2,2,128,256]{3,2,1,0:T(8,128)(2,1)S(1)} %add_convert_fusion), kind=kLoop, calls=%fused_computation.2 | loop fusion | bytes 524288 | tf_op jit(solution)/shard_map/squeeze | solution.py:264
  (4 shorter events, 0.0 us)
Async XLA Ops:
  1.6 10.4 %collective-permute-start = (bf16[2,2,128,256]{3,2,1,0:T(8,128)(2,1)S(1)}, bf16[2,2,128,256]{3,2,1,0:T(8,128)(2,1)S(1)}, u32[]{:S(2)}, u32[]{:S(2)}) collective-permute-start(bf16[2,2,128,256]{3,2,1,0:T(8,128)(2,1)S(1)} %pad_maximum_fusion), channel_id=1, source_target_pairs={{0,2},{2,4},{4,6},{6,8},{8,10},{10,12},{12,14},{1,3},{3,5},{5,7},{... | collective-permute-start | bytes 786440 | tf_op jit(solution)/shard_map/ppermute | solution.py:32
  12.1 0.7 %copy-start = (bf16[2,2,128,256]{3,2,1,0:T(8,128)(2,1)}, bf16[2,2,128,256]{3,2,1,0:T(8,128)(2,1)S(1)}, u32[]{:S(2)}) copy-start(bf16[2,2,128,256]{3,2,1,0:T(8,128)(2,1)S(1)} %collective-permute-done.hk_ref.hv_ref) | copy-start | bytes 786436
  24.6 1.3 %copy-start.1 = (f32[1,128]{1,0:T(1,128)S(1)}, f32[1,128]{1,0:T(1,128)}, u32[]{:S(2)}) copy-start(f32[1,128]{1,0:T(1,128)} %get-tuple-element.11) | copy-start | bytes 1540
  24.6 19.8 %collective-permute-start.1 = (bf16[2,2,128,256]{3,2,1,0:T(8,128)(2,1)}, bf16[2,2,128,256]{3,2,1,0:T(8,128)(2,1)S(1)}, u32[]{:S(2)}, u32[]{:S(2)}) collective-permute-start(bf16[2,2,128,256]{3,2,1,0:T(8,128)(2,1)} %get-tuple-element.10), channel_id=1, source_target_pairs={{2,0},{4,2},{6,4},{8,6},{10,8},{12,10},{14,12},{3,1},{5,3},{7,5},{... | collective-permute-start | bytes 786440 | tf_op jit(solution)/shard_map/ppermute | solution.py:32
  25.9 3.6 %collective-permute-start.2 = (f32[32]{0:T(128)S(1)}, f32[32]{0:T(128)S(1)}, u32[]{:S(2)}, u32[]{:S(2)}) collective-permute-start(f32[32]{0:T(128)S(1)} %slice_bitcast_fusion.2), channel_id=1, source_target_pairs={{0,16},{16,0},{1,17},{17,1},{2,18},{18,2},{3,19},{19,3},{4,20},{20... | collective-permute-start | bytes 392 | tf_op jit(solution)/shard_map/ppermute | solution.py:43
  29.5 5.2 %collective-permute-start.3 = (f32[32]{0:T(128)S(1)}, f32[32]{0:T(128)S(1)}, u32[]{:S(2)}, u32[]{:S(2)}) collective-permute-start(f32[32]{0:T(128)S(1)} %fusion), channel_id=1, source_target_pairs={{0,2},{2,0},{4,6},{6,4},{8,10},{10,8},{12,14},{14,12},{1,3},{3,1},... | collective-permute-start | bytes 392 | tf_op jit(solution)/shard_map/ppermute | solution.py:43
  34.7 4.5 %collective-permute-start.4 = (f32[32]{0:T(128)S(1)}, f32[32]{0:T(128)S(1)}, u32[]{:S(2)}, u32[]{:S(2)}) collective-permute-start(f32[32]{0:T(128)S(1)} %add.17), channel_id=1, source_target_pairs={{0,4},{2,6},{4,0},{6,2},{8,12},{10,14},{12,8},{14,10},{1,5},{3,7},... | collective-permute-start | bytes 392 | tf_op jit(solution)/shard_map/ppermute | solution.py:43
  39.2 4.6 %collective-permute-start.5 = (f32[32]{0:T(128)S(1)}, f32[32]{0:T(128)S(1)}, u32[]{:S(2)}, u32[]{:S(2)}) collective-permute-start(f32[32]{0:T(128)S(1)} %add.18), channel_id=1, source_target_pairs={{0,8},{2,10},{4,12},{6,14},{8,0},{10,2},{12,4},{14,6},{1,9},{3,11}... | collective-permute-start | bytes 392 | tf_op jit(solution)/shard_map/ppermute | solution.py:43

commit v2 on v1

v2 whole, which is shorter than its diff:
```python
import functools
import math

import jax
import jax.numpy as jnp
from jax import lax
from jax.experimental import pallas as pl
from jax.experimental.pallas import tpu as pltpu
from jax.sharding import PartitionSpec as P

HEAD_DIMENSION = 64
WINDOW_LENGTH = 128
LANES = 128

masked_score = -1e30

dot_nt = functools.partial(
    lax.dot_general,
    dimension_numbers=(((1,), (1,)), ((), ())),
    preferred_element_type=jnp.float32,
)
dot_nn = functools.partial(
    lax.dot_general,
    dimension_numbers=(((1,), (0,)), ((), ())),
    preferred_element_type=jnp.float32,
)


def passed_along(value, axis, steps):
    count = lax.axis_size(axis)
    first, last = (max(0, -steps), min(count, count - steps))
    return lax.ppermute(value, axis, [(source, source + steps) for source in range(first, last)])


def total_over(value, axes):
    for axis in axes:
        count = lax.axis_size(axis)
        if count & (count - 1):
            value = lax.psum(value, axis)
            continue
        step = 1
        while step < count:
            value = value + lax.ppermute(value, axis, [(i, i ^ step) for i in range(count)])
            step *= 2
    return value


def lane_half(rows):
    return lax.broadcasted_iota(jnp.int32, (rows, LANES), 1) < HEAD_DIMENSION


def half_pair(tile, which):
    low = lane_half(WINDOW_LENGTH)
    wide = tile.astype(jnp.float32)
    if which == 0:
        lo = jnp.where(low, wide, 0.0)
        hi = pltpu.roll(lo, HEAD_DIMENSION, 1)
    else:
        hi = jnp.where(low, 0.0, wide)
        lo = pltpu.roll(hi, HEAD_DIMENSION, 1)
    return jnp.concatenate([lo, hi], axis=0).astype(jnp.bfloat16)


def twice(tile):
    return jnp.concatenate([tile, tile], axis=1)


def lower_triangle():
    key_row = lax.broadcasted_iota(jnp.int32, (WINDOW_LENGTH, LANES), 0)
    query_lane = lax.broadcasted_iota(jnp.int32, (WINDOW_LENGTH, LANES), 1)
    return key_row <= query_lane


def biases(starts_ref, counts_ref, seq, block):
    base = block * WINDOW_LENGTH
    query = base + lax.broadcasted_iota(jnp.int32, (8, LANES), 1)
    oldest = jnp.zeros((8, LANES), jnp.int32)
    for entry in range(starts_ref.shape[1]):
        start = starts_ref[seq, entry]
        oldest = jnp.maximum(oldest, jnp.where(start <= query, start, 0))
    oldest = jnp.broadcast_to(oldest[:1], (WINDOW_LENGTH, LANES))
    key_row = lax.broadcasted_iota(jnp.int32, (WINDOW_LENGTH, LANES), 0)
    lower = lower_triangle()
    own_limit = counts_ref[seq, block]
    prev_limit = counts_ref[seq, jnp.maximum(block - 1, 0)]
    own = lower & (key_row + base >= oldest) & (key_row < own_limit)
    prev = (
        jnp.logical_not(lower)
        & (key_row + (base - WINDOW_LENGTH) >= oldest)
        & (key_row < prev_limit)
    )
    return jnp.where(own, 0.0, masked_score), jnp.where(prev, 0.0, masked_score)


class Shape:
    def __init__(self, seqs, heads_kv, group):
        self.seqs, self.heads_kv, self.group = seqs, heads_kv, group
        self.quads = group // 4
        self.tiles = heads_kv * group // 2

    def cat(self, ref, seq, head_kv, quads):
        first = head_kv * self.group // 2 + quads.start * 2
        count = 2 * len(quads)
        return ref[seq, first : first + count].reshape(count * WINDOW_LENGTH, LANES)

    def kv_tile(self, ref, seq, head_kv):
        at = head_kv // 2 * LANES
        return ref[seq, :, at : at + LANES]


def pack_kernel(k_ref, v_ref, out_ref, sems):
    copies = [
        pltpu.make_async_copy(ref, out_ref.at[kind], sems.at[kind])
        for kind, ref in enumerate((k_ref, v_ref))
    ]
    for copy in copies:
        copy.start()
    for copy in copies:
        copy.wait()


def own_kernel(
    sinks_hbm,
    starts_hbm,
    counts_hbm,
    q_hbm,
    g_hbm,
    kv_ref,
    q_ref,
    g_ref,
    s_ref,
    dp_ref,
    bias_ref,
    sink_ref,
    sinks_ref,
    starts_ref,
    counts_ref,
    small_sems,
    sems,
    *,
    shape,
):
    scaling = HEAD_DIMENSION**-0.5
    block = lax.axis_index("ctx")
    small = [
        pltpu.make_async_copy(source, target, small_sems.at[i])
        for i, (source, target) in enumerate(
            ((starts_hbm, starts_ref), (counts_hbm, counts_ref), (sinks_hbm, sinks_ref))
        )
    ]
    for copy in small:
        copy.start()
    copies = {}
    for seq in range(shape.seqs):
        for tile in range(shape.tiles):
            for kind, (source, target) in enumerate(((q_hbm, q_ref), (g_hbm, g_ref))):
                copy = pltpu.make_async_copy(
                    source.at[seq, :, tile * LANES : (tile + 1) * LANES],
                    target.at[seq, tile],
                    sems.at[seq, tile, kind],
                )
                copy.start()
                copies[seq, tile, kind] = copy
    for copy in small:
        copy.wait()
    for head in range(sink_ref.shape[0]):
        sink_ref[head : head + 1, :] = jnp.full((1, LANES), sinks_ref[head] / scaling, jnp.float32)
    for seq in range(shape.seqs):
        own, prev = biases(starts_ref, counts_ref, seq, block)
        bias_ref[seq] = prev
        own = twice(own)
        own = jnp.concatenate([own, own], axis=0)
        for head_kv in range(shape.heads_kv):
            keys = half_pair(shape.kv_tile(kv_ref.at[0], seq, head_kv), head_kv % 2)
            vals = half_pair(shape.kv_tile(kv_ref.at[1], seq, head_kv), head_kv % 2)
            for quad in range(shape.quads):
                at = head_kv * shape.group // 2 + quad * 2
                for kind in range(2):
                    for tile in (at, at + 1):
                        copies[seq, tile, kind].wait()
                some = range(quad, quad + 1)
                s_ref[seq, head_kv, quad] = dot_nt(keys, shape.cat(q_ref, seq, head_kv, some)) + own
                dp_ref[seq, head_kv, quad] = dot_nt(vals, shape.cat(g_ref, seq, head_kv, some))


def softmax_kernel(
    sinks_ref, q_ref, g_ref, halo_ref, s_ref, dp_ref, bias_ref, p_ref, ds_ref, sink_ref, sink_rows, *, shape
):
    scaling = HEAD_DIMENSION**-0.5
    to_exp2 = scaling * math.log2(math.e)
    lower = twice(lower_triangle())
    sink_rows[...] = jnp.zeros_like(sink_rows)
    for seq in range(shape.seqs):
        bias = twice(bias_ref[seq])
        for head_kv in range(shape.heads_kv):
            keys = half_pair(shape.kv_tile(halo_ref.at[0], seq, head_kv), head_kv % 2)
            vals = half_pair(shape.kv_tile(halo_ref.at[1], seq, head_kv), head_kv % 2)
            for quad in range(shape.quads):
                some = range(quad, quad + 1)
                scores = dot_nt(keys, shape.cat(q_ref, seq, head_kv, some))
                dprobs = dot_nt(vals, shape.cat(g_ref, seq, head_kv, some))
                for half in range(2):
                    rows = slice(half * WINDOW_LENGTH, (half + 1) * WINDOW_LENGTH)
                    head = head_kv * shape.group + quad * 4 + half
                    sink = jnp.concatenate(
                        [sinks_ref[head : head + 1, :], sinks_ref[head + 2 : head + 3, :]], axis=1
                    )
                    s = jnp.maximum(s_ref[seq, head_kv, quad, rows], scores[rows] + bias)
                    top = jnp.maximum(jnp.max(s, axis=0, keepdims=True), sink)
                    power = jnp.exp2((s - top) * to_exp2)
                    sink_power = jnp.exp2((sink - top) * to_exp2)
                    inverse = 1.0 / (jnp.sum(power, axis=0, keepdims=True) + sink_power)
                    dprob = jnp.where(lower, dp_ref[seq, head_kv, quad, rows], dprobs[rows])
                    delta = jnp.sum(power * dprob, axis=0, keepdims=True) * inverse
                    prob = power * inverse
                    p_ref[seq, head_kv, quad, rows] = prob.astype(jnp.bfloat16)
                    ds_ref[seq, head_kv, quad, rows] = (prob * (dprob - delta)).astype(jnp.bfloat16)
                    sink_term = sink_power * inverse * delta
                    sink_rows[head : head + 1, :] += sink_term[:, :LANES]
                    sink_rows[head + 2 : head + 3, :] += sink_term[:, LANES:]
    sink_ref[...] = -jnp.sum(sink_rows[...].T, axis=0, keepdims=True)


def kv_grad_kernel(q_ref, g_ref, p_ref, ds_ref, out_ref, *, shape, own):
    scaling = HEAD_DIMENSION**-0.5
    lower = twice(lower_triangle())
    keep = jnp.where(lower, 1.0 if own else 0.0, 0.0 if own else 1.0).astype(jnp.bfloat16)
    low = lane_half(WINDOW_LENGTH)
    for seq in range(shape.seqs):
        for kind, (weight_ref, wide_ref, factor) in enumerate(
            ((ds_ref, q_ref, scaling), (p_ref, g_ref, 1.0))
        ):
            for pair in range(shape.heads_kv // 2):
                sums = []
                for head_kv in (2 * pair, 2 * pair + 1):
                    right = shape.cat(wide_ref, seq, head_kv, range(shape.quads))
                    left = jnp.concatenate(
                        [
                            jnp.concatenate(
                                [
                                    weight_ref[
                                        seq, head_kv, quad, half * WINDOW_LENGTH : (half + 1) * WINDOW_LENGTH
                                    ]
                                    * keep
                                    for quad in range(shape.quads)
                                ],
                                axis=1,
                            )
                            for half in range(2)
                        ],
                        axis=0,
                    )
                    both = dot_nn(left, right)
                    sums.append((both[:WINDOW_LENGTH], both[WINDOW_LENGTH:]))
                (lo0, hi0), (lo1, hi1) = sums
                grad = jnp.where(low, lo0, hi1) + pltpu.roll(
                    jnp.where(low, lo1, hi0), HEAD_DIMENSION, 1
                )
                out_ref[kind, seq, :, pair * LANES : (pair + 1) * LANES] = (grad * factor).astype(
                    out_ref.dtype
                )


def query_grad_kernel(kv_ref, halo_ref, ds_ref, dq_ref, *, shape):
    scaling = HEAD_DIMENSION**-0.5
    lower_low = jnp.where(twice(lower_triangle()), 1.0, 0.0).astype(jnp.bfloat16)
    for seq in range(shape.seqs):
        for head_kv in range(shape.heads_kv):
            rows = slice(head_kv % 2 * HEAD_DIMENSION, (head_kv % 2 + 1) * HEAD_DIMENSION)
            keys_t = jnp.concatenate(
                [
                    shape.kv_tile(kv_ref.at[0], seq, head_kv).T[rows],
                    shape.kv_tile(halo_ref.at[0], seq, head_kv).T[rows],
                ],
                axis=1,
            )
            for quad in range(shape.quads):
                parts = []
                for half in range(2):
                    dscore = ds_ref[
                        seq, head_kv, quad, half * WINDOW_LENGTH : (half + 1) * WINDOW_LENGTH
                    ]
                    own = dscore * lower_low
                    parts.append(
                        dot_nn(keys_t, jnp.concatenate([own, dscore - own], axis=0)) * scaling
                    )
                for part in range(2):
                    lanes = slice(part * LANES, (part + 1) * LANES)
                    at = (head_kv * shape.group // 2 + quad * 2 + part) * LANES
                    tile = jnp.concatenate([parts[0][:, lanes], parts[1][:, lanes]], axis=0)
                    dq_ref[seq, :, at : at + LANES] = tile.astype(jnp.bfloat16).T


def add_kernel(own_ref, edge_ref, dk_ref, dv_ref):
    dk_ref[...] = (own_ref[0] + edge_ref[0].astype(jnp.float32)).astype(jnp.bfloat16)
    dv_ref[...] = (own_ref[1] + edge_ref[1].astype(jnp.float32)).astype(jnp.bfloat16)


VMEM = pl.BlockSpec(memory_space=pltpu.VMEM)
HBM = pl.BlockSpec(memory_space=pltpu.HBM)


def in_hbm(value):
    return pltpu.with_memory_space_constraint(value, pltpu.HBM)


def call(kernel, in_specs, outs, flops, scratch=(), **settings):
    return pl.pallas_call(
        functools.partial(kernel, **settings),
        in_specs=in_specs,
        out_specs=jax.tree.map(lambda _: VMEM, outs),
        out_shape=outs,
        scratch_shapes=scratch,
        cost_estimate=pl.CostEstimate(flops=flops, transcendentals=0, bytes_accessed=1024),
        compiler_params=pltpu.CompilerParams(vmem_limit_bytes=24 * 2**20),
        name=kernel.__name__,
    )


def local(queries, keys, values, output_gradient, sinks, doc_starts, valid_counts):
    seq_count, row_count, query_width = queries.shape
    kv_width = keys.shape[2]
    heads_kv = kv_width // HEAD_DIMENSION
    head_count = sinks.shape[0]
    shape = Shape(seq_count, heads_kv, head_count // heads_kv)
    assert row_count == WINDOW_LENGTH
    product = 2 * seq_count * head_count * WINDOW_LENGTH * WINDOW_LENGTH * HEAD_DIMENSION
    tiles = (seq_count, heads_kv, shape.quads, 2 * WINDOW_LENGTH, 2 * LANES)
    padded_heads = -(-head_count // LANES) * LANES
    f32, bf16 = jnp.float32, jnp.bfloat16
    new = jax.ShapeDtypeStruct

    both = call(
        pack_kernel,
        [HBM] * 2,
        new((2,) + keys.shape, bf16),
        product // 8,
        scratch=[pltpu.SemaphoreType.DMA((2,))],
    )(in_hbm(keys), in_hbm(values))
    halo = passed_along(both, "ctx", 1)
    wide_tiles = (seq_count, shape.tiles, WINDOW_LENGTH, LANES)
    q_tiles, g_tiles, scores, dprobs, bias, sink_lanes = call(
        own_kernel,
        [HBM] * 5 + [VMEM],
        [
            new(wide_tiles, bf16),
            new(wide_tiles, bf16),
            new(tiles, f32),
            new(tiles, f32),
            new((seq_count, WINDOW_LENGTH, LANES), f32),
            new((head_count, LANES), f32),
        ],
        2 * product,
        scratch=[
            pltpu.SMEM(sinks.shape, f32),
            pltpu.SMEM(doc_starts.shape, jnp.int32),
            pltpu.SMEM(valid_counts.shape, jnp.int32),
            pltpu.SemaphoreType.DMA((3,)),
            pltpu.SemaphoreType.DMA((seq_count, shape.tiles, 2)),
        ],
        shape=shape,
    )(*map(in_hbm, (sinks, doc_starts, valid_counts, queries, output_gradient)), both)
    prob, dscore, sink_part = call(
        softmax_kernel,
        [VMEM] * 7,
        [new(tiles, bf16), new(tiles, bf16), new((1, padded_heads), f32)],
        2 * product,
        scratch=[pltpu.VMEM((padded_heads, LANES), f32)],
        shape=shape,
    )(sink_lanes, q_tiles, g_tiles, halo, scores, dprobs, bias)
    prev = call(
        kv_grad_kernel, [VMEM] * 4, new((2,) + keys.shape, bf16), 2 * product, shape=shape, own=False
    )(q_tiles, g_tiles, prob, dscore)
    edge = passed_along(prev, "ctx", -1)
    query_grad = call(
        query_grad_kernel, [VMEM] * 3, new(queries.shape, bf16), 2 * product, shape=shape
    )(both, halo, dscore)
    own = call(
        kv_grad_kernel, [VMEM] * 4, new((2,) + keys.shape, f32), 2 * product, shape=shape, own=True
    )(q_tiles, g_tiles, prob, dscore)
    key_grad, value_grad = call(
        add_kernel, [VMEM] * 2, [new(keys.shape, bf16), new(keys.shape, bf16)], product // 8
    )(own, edge)
    sink_grad = total_over(sink_part, ("dp", "ctx"))[0, :head_count]
    return (query_grad, key_grad, value_grad, sink_grad)


def solution(mesh):
    placed = (
        P("dp", "ctx", "tp"),
        P("dp", "ctx", "tp"),
        P("dp", "ctx", "tp"),
        P("dp", "ctx", "tp"),
        P("tp"),
        P("dp", None),
        P("dp", None),
    )
    return jax.shard_map(
        local,
        mesh=mesh,
        in_specs=placed,
        out_specs=(P("dp", "ctx", "tp"), P("dp", "ctx", "tp"), P("dp", "ctx", "tp"), P("tp")),
        check_vma=False,
    )
```

time: 46.4 us -> 37.8 us (0.81)
  waiting for transfers between devices: 12.7 us -> 5.05 us
  Pallas kernels: 11.8 us -> 14.8 us
  other arithmetic: 2.63 us -> 0.01 us
  local copies, waits for them, and re-layouts: 1.43 us -> 0.52 us
  starting transfers between devices: 16.9 us -> 16.4 us
    ppermute x2, waiting for transfers between devices: 5.53 us -> 0.06 us  [passed_along(): lax.ppermute(value, axis, [(source, source + steps) for source in range(f...]
    pallas_call x1 -> x7, Pallas kernels: 11.8 us -> 14.8 us  [the longest x1 5.47 us: local(): call(own_kernel, [HBM] * 5 + [VMEM], [new(wide_tiles, bf16), new(wide_til...]
    ppermute x4, waiting for transfers between devices: 7.2 us -> 4.99 us  [total_over(): lax.ppermute(value, axis, [(i, i ^ step) for i in range(count)])]
    convert_element_type x1 -> x0, other arithmetic: 1.11 us -> none  [local(): total = (own + edge.astype(jnp.float32)).astype(jnp.bfloat16)]
    another operation x1 -> x0, other arithmetic: 1 us -> none  [local(): halo = passed_along(jnp.stack([keys, values]), 'ctx', 1)]
    unnamed x4 -> x0, local copies, waits for them, and re-layouts: 0.71 us -> none
    add x4, other arithmetic: 0.52 us -> 0.01 us  [total_over(): value + lax.ppermute(value, axis, [(i, i ^ step) for i in range(count)])]
    ppermute x4, starting transfers between devices: 10.7 us -> 10.2 us  [total_over(): lax.ppermute(value, axis, [(i, i ^ step) for i in range(count)])]
  transfers between devices with their start and end apart: 6 -> 6, of which waited for: 5 -> 3; matrix products, arithmetic and copies ran while one was open for 1% -> 1% of each run, Pallas kernels for 0% -> 27%
where the time goes in v2:
time: 37.8 us; the launch traced here: 37.5 us
  starting transfers between devices  16.4 us (43%)
  Pallas kernels  14.8 us (39%)
  waiting for transfers between devices  5.05 us (13%)
  between operations  0.7 us (2%)
  local copies, waits for them, and re-layouts  0.52 us (1%)
    ppermute x4, starting transfers between devices, total_over(): lax.ppermute(value, axis, [(i, i ^ step) for i in range(count)])  10.2 us
    ppermute x2, starting transfers between devices, passed_along(): lax.ppermute(value, axis, [(source, source + steps) for source in range(f...  6.18 us
    pallas_call x1, Pallas kernels, local(): call(own_kernel, [HBM] * 5 + [VMEM], [new(wide_tiles, bf16), new(wide_til...  5.47 us
    ppermute x4, waiting for transfers between devices, total_over(): lax.ppermute(value, axis, [(i, i ^ step) for i in range(count)])  4.99 us
    pallas_call x1, Pallas kernels, local(): call(softmax_kernel, [VMEM] * 7, [new(tiles, bf16), new(tiles, bf16), new...  3.11 us
    pallas_call x1, Pallas kernels, local(): call(query_grad_kernel, [VMEM] * 3, new(queries.shape, bf16), 2 * product...  1.92 us
    pallas_call x1, Pallas kernels, local(): call(kv_grad_kernel, [VMEM] * 4, new((2,) + keys.shape, f32), 2 * product...  1.3 us
    pallas_call x1, Pallas kernels, local(): call(kv_grad_kernel, [VMEM] * 4, new((2,) + keys.shape, bf16), 2 * produc...  1.3 us
  transfers between devices with their start and end apart: 6, of which 3 were waited for; matrix products, arithmetic and copies ran while one was open for 1% of the time, Pallas kernels for 27%

profile of v2, /device:TPU:0, one launch (start us, length us, event | category | flops | bytes accessed | tf_op | source)
XLA Modules:
  0.0 37.5 jit_solution(997322691210958059)
XLA Ops:
  0.6 1.0 %pack_kernel.1.kv_ref = bf16[2,2,128,256]{3,2,1,0:T(8,128)(2,1)S(1)} custom-call(bf16[2,128,256]{2,1,0:T(8,128)(2,1)} %k_ref.1, bf16[2,128,256]{2,1,0:T(8,128)(2,1)} %v_ref.1), custom_call_target="tpu_custom_call" | custom-call | flops 16777216 | bytes 1024 | tf_op jit(solution)/shard_map/pack_kernel/pallas_call | solution.py:333
  1.6 4.9 %collective-permute-start = (bf16[2,2,128,256]{3,2,1,0:T(8,128)(2,1)S(1)}, bf16[2,2,128,256]{3,2,1,0:T(8,128)(2,1)S(1)}, u32[]{:S(2)}, u32[]{:S(2)}) collective-permute-start(bf16[2,2,128,256]{3,2,1,0:T(8,128)(2,1)S(1)} %pack_kernel.1.kv_ref), channel_id=1, source_target_pairs={{0,2},{2,4},{4,6},{6,8},{8,10},{10,12},{12,14},{1,3},{3,5},{5,7},{... | collective-permute-start | bytes 786440 | tf_op jit(solution)/shard_map/ppermute | solution.py:32
  6.5 5.5 %own_kernel.1 = (bf16[2,16,128,128]{3,2,1,0:T(8,128)(2,1)S(1)}, bf16[2,16,128,128]{3,2,1,0:T(8,128)(2,1)S(1)}, f32[2,4,2,256,256]{4,3,2,1,0:T(8,128)S(1)}, f32[2...) custom-call(f32[32]{0:T(128)} %sinks_hbm.1, s32[2,64]{1,0:T(2,128)} %starts_hbm.1, ...), custom_call_target="tpu_custom_call" | custom-call | flops 268435456 | bytes 1024 | tf_op jit(solution)/shard_map/own_kernel/pallas_call | solution.py:342
  12.0 0.1 collective-permute-done.halo_ref
  12.1 3.1 %softmax_kernel.1 = (bf16[2,4,2,256,256]{4,3,2,1,0:T(8,128)(2,1)S(1)}, bf16[2,4,2,256,256]{4,3,2,1,0:T(8,128)(2,1)S(1)}, f32[1,128]{1,0:T(1,128)S(1)}) custom-call(f32[32,128]{1,0:T(8,128)S(1)} %get-tuple-element.15.sinks_ref, bf16[2,16,128,128]{3,2,1,0:T(8,128)(2,1)S(1)} %get-tuple-element.16.q_ref, bf16[2,16,128,128]{3,2,1,0:T(8,128)(2,1)S(1)} %get-tuple-element.17.g_ref, ...), custom_call_target="tpu_custom_call" | custom-call | flops 268435456 | bytes 1024 | tf_op jit(solution)/shard_map/softmax_kernel/pallas_call | solution.py:363
  15.2 1.6 %collective-permute-start.2 = (f32[1,128]{1,0:T(1,128)S(1)}, f32[1,128]{1,0:T(1,128)S(1)}, u32[]{:S(2)}, u32[]{:S(2)}) collective-permute-start(f32[1,128]{1,0:T(1,128)S(1)} %get-tuple-element.25), channel_id=1, source_target_pairs={{0,16},{16,0},{1,17},{17,1},{2,18},{18,2},{3,19},{19,3},{4,20},{20... | collective-permute-start | bytes 1544 | tf_op jit(solution)/shard_map/ppermute | solution.py:43
  16.8 2.0 %collective-permute-done.2 = f32[1,128]{1,0:T(1,128)S(1)} collective-permute-done((f32[1,128]{1,0:T(1,128)S(1)}, f32[1,128]{1,0:T(1,128)S(1)}, u32[]{:S(2)}, u32[]{:S(2)}) %collective-permute-start.2) | collective-permute-done | bytes 544 | tf_op jit(solution)/shard_map/ppermute | solution.py:43
  18.8 2.5 %collective-permute-start.3 = (f32[1,128]{1,0:T(1,128)S(1)}, f32[1,128]{1,0:T(1,128)S(1)}, u32[]{:S(2)}, u32[]{:S(2)}) collective-permute-start(f32[1,128]{1,0:T(1,128)S(1)} %add.12), channel_id=1, source_target_pairs={{0,2},{2,0},{4,6},{6,4},{8,10},{10,8},{12,14},{14,12},{1,3},{3,1},... | collective-permute-start | bytes 1544 | tf_op jit(solution)/shard_map/ppermute | solution.py:43
  21.3 1.3 %kv_grad_kernel.3 = bf16[2,2,128,256]{3,2,1,0:T(8,128)(2,1)S(1)} custom-call(bf16[2,16,128,128]{3,2,1,0:T(8,128)(2,1)S(1)} %get-tuple-element.16.q_ref, bf16[2,16,128,128]{3,2,1,0:T(8,128)(2,1)S(1)} %get-tuple-element.17.g_ref, bf16[2,4,2,256,256]{4,3,2,1,0:T(8,128)(2,1)S(1)} %get-tuple-element.22.p_ref, ...), custom_call_target="tpu_custom_call" | custom-call | flops 268435456 | bytes 1024 | tf_op jit(solution)/shard_map/kv_grad_kernel/pallas_call | solution.py:371
  22.6 1.3 %collective-permute-start.1 = (bf16[2,2,128,256]{3,2,1,0:T(8,128)(2,1)S(1)}, bf16[2,2,128,256]{3,2,1,0:T(8,128)(2,1)S(1)}, u32[]{:S(2)}, u32[]{:S(2)}) collective-permute-start(bf16[2,2,128,256]{3,2,1,0:T(8,128)(2,1)S(1)} %kv_grad_kernel.3), channel_id=1, source_target_pairs={{2,0},{4,2},{6,4},{8,6},{10,8},{12,10},{14,12},{3,1},{5,3},{7,5},{... | collective-permute-start | bytes 786440 | tf_op jit(solution)/shard_map/ppermute | solution.py:32
  23.9 0.0 collective-permute-done.3
  23.9 2.3 %collective-permute-start.4 = (f32[1,128]{1,0:T(1,128)S(1)}, f32[1,128]{1,0:T(1,128)S(1)}, u32[]{:S(2)}, u32[]{:S(2)}) collective-permute-start(f32[1,128]{1,0:T(1,128)S(1)} %add.13), channel_id=1, source_target_pairs={{0,4},{2,6},{4,0},{6,2},{8,12},{10,14},{12,8},{14,10},{1,5},{3,7},... | collective-permute-start | bytes 1544 | tf_op jit(solution)/shard_map/ppermute | solution.py:43
  26.2 1.3 %kv_grad_kernel.2.own_ref = f32[2,2,128,256]{3,2,1,0:T(8,128)S(1)} custom-call(bf16[2,16,128,128]{3,2,1,0:T(8,128)(2,1)S(1)} %get-tuple-element.16.q_ref, bf16[2,16,128,128]{3,2,1,0:T(8,128)(2,1)S(1)} %get-tuple-element.17.g_ref, bf16[2,4,2,256,256]{4,3,2,1,0:T(8,128)(2,1)S(1)} %get-tuple-element.22.p_ref, ...), custom_call_target="tpu_custom_call" | custom-call | flops 268435456 | bytes 1024 | tf_op jit(solution)/shard_map/kv_grad_kernel/pallas_call | solution.py:378
  27.5 2.9 %collective-permute-done.4 = f32[1,128]{1,0:T(1,128)S(1)} collective-permute-done((f32[1,128]{1,0:T(1,128)S(1)}, f32[1,128]{1,0:T(1,128)S(1)}, u32[]{:S(2)}, u32[]{:S(2)}) %collective-permute-start.4) | collective-permute-done | bytes 544 | tf_op jit(solution)/shard_map/ppermute | solution.py:43
  30.4 3.9 %collective-permute-start.5 = (f32[1,128]{1,0:T(1,128)S(1)}, f32[1,128]{1,0:T(1,128)S(1)}, u32[]{:S(2)}, u32[]{:S(2)}) collective-permute-start(f32[1,128]{1,0:T(1,128)S(1)} %add.14), channel_id=1, source_target_pairs={{0,8},{2,10},{4,12},{6,14},{8,0},{10,2},{12,4},{14,6},{1,9},{3,11}... | collective-permute-start | bytes 1544 | tf_op jit(solution)/shard_map/ppermute | solution.py:43
  34.3 1.9 %query_grad_kernel.1 = bf16[2,128,2048]{2,1,0:T(8,128)(2,1)} custom-call(bf16[2,2,128,256]{3,2,1,0:T(8,128)(2,1)S(1)} %pack_kernel.1.kv_ref, bf16[2,2,128,256]{3,2,1,0:T(8,128)(2,1)S(1)} %collective-permute-done.halo_ref, bf16[2,4,2,256,256]{4,3,2,1,0:T(8,128)(2,1)S(1)} %get-tuple-element.21.ds_ref), custom_call_target="tpu_custom_call" | custom-call | flops 268435456 | bytes 1024 | tf_op jit(solution)/shard_map/query_grad_kernel/pallas_call | solution.py:375
  36.3 0.0 collective-permute-done.5
  36.3 0.5 %slice_bitcast_fusion = f32[32]{0:T(128)} fusion(f32[1,128]{1,0:T(1,128)S(1)} %add.15), kind=kLoop, calls=%fused_computation | loop fusion | bytes 256 | tf_op jit(solution)/shard_map/squeeze | solution.py:384
  36.8 0.0 collective-permute-done.1.edge_ref
  36.8 0.7 %add_kernel.1 = (bf16[2,128,256]{2,1,0:T(8,128)(2,1)}, bf16[2,128,256]{2,1,0:T(8,128)(2,1)}) custom-call(f32[2,2,128,256]{3,2,1,0:T(8,128)S(1)} %kv_grad_kernel.2.own_ref, bf16[2,2,128,256]{3,2,1,0:T(8,128)(2,1)S(1)} %collective-permute-done.1.edge_ref), custom_call_target="tpu_custom_call" | custom-call | flops 16777216 | bytes 1024 | tf_op jit(solution)/shard_map/add_kernel/pallas_call | solution.py:381
  (4 shorter events, 0.0 us)
Async XLA Ops:
  1.6 10.4 %collective-permute-start = (bf16[2,2,128,256]{3,2,1,0:T(8,128)(2,1)S(1)}, bf16[2,2,128,256]{3,2,1,0:T(8,128)(2,1)S(1)}, u32[]{:S(2)}, u32[]{:S(2)}) collective-permute-start(bf16[2,2,128,256]{3,2,1,0:T(8,128)(2,1)S(1)} %pack_kernel.1.kv_ref), channel_id=1, source_target_pairs={{0,2},{2,4},{4,6},{6,8},{8,10},{10,12},{12,14},{1,3},{3,5},{5,7},{... | collective-permute-start | bytes 786440 | tf_op jit(solution)/shard_map/ppermute | solution.py:32
  15.2 3.6 %collective-permute-start.2 = (f32[1,128]{1,0:T(1,128)S(1)}, f32[1,128]{1,0:T(1,128)S(1)}, u32[]{:S(2)}, u32[]{:S(2)}) collective-permute-start(f32[1,128]{1,0:T(1,128)S(1)} %get-tuple-element.25), channel_id=1, source_target_pairs={{0,16},{16,0},{1,17},{17,1},{2,18},{18,2},{3,19},{19,3},{4,20},{20... | collective-permute-start | bytes 1544 | tf_op jit(solution)/shard_map/ppermute | solution.py:43
  18.8 5.1 %collective-permute-start.3 = (f32[1,128]{1,0:T(1,128)S(1)}, f32[1,128]{1,0:T(1,128)S(1)}, u32[]{:S(2)}, u32[]{:S(2)}) collective-permute-start(f32[1,128]{1,0:T(1,128)S(1)} %add.12), channel_id=1, source_target_pairs={{0,2},{2,0},{4,6},{6,4},{8,10},{10,8},{12,14},{14,12},{1,3},{3,1},... | collective-permute-start | bytes 1544 | tf_op jit(solution)/shard_map/ppermute | solution.py:43
  22.6 14.2 %collective-permute-start.1 = (bf16[2,2,128,256]{3,2,1,0:T(8,128)(2,1)S(1)}, bf16[2,2,128,256]{3,2,1,0:T(8,128)(2,1)S(1)}, u32[]{:S(2)}, u32[]{:S(2)}) collective-permute-start(bf16[2,2,128,256]{3,2,1,0:T(8,128)(2,1)S(1)} %kv_grad_kernel.3), channel_id=1, source_target_pairs={{2,0},{4,2},{6,4},{8,6},{10,8},{12,10},{14,12},{3,1},{5,3},{7,5},{... | collective-permute-start | bytes 786440 | tf_op jit(solution)/shard_map/ppermute | solution.py:32
  23.9 6.5 %collective-permute-start.4 = (f32[1,128]{1,0:T(1,128)S(1)}, f32[1,128]{1,0:T(1,128)S(1)}, u32[]{:S(2)}, u32[]{:S(2)}) collective-permute-start(f32[1,128]{1,0:T(1,128)S(1)} %add.13), channel_id=1, source_target_pairs={{0,4},{2,6},{4,0},{6,2},{8,12},{10,14},{12,8},{14,10},{1,5},{3,7},... | collective-permute-start | bytes 1544 | tf_op jit(solution)/shard_map/ppermute | solution.py:43
  30.4 5.8 %collective-permute-start.5 = (f32[1,128]{1,0:T(1,128)S(1)}, f32[1,128]{1,0:T(1,128)S(1)}, u32[]{:S(2)}, u32[]{:S(2)}) collective-permute-start(f32[1,128]{1,0:T(1,128)S(1)} %add.14), channel_id=1, source_target_pairs={{0,8},{2,10},{4,12},{6,14},{8,0},{10,2},{12,4},{14,6},{1,9},{3,11}... | collective-permute-start | bytes 1544 | tf_op jit(solution)/shard_map/ppermute | solution.py:43
